TPU v7x, 32 devices: a whole 2x2x4 slice. The times are simulated.
32 devices in a mesh: row: 4 (over z), col: 4 (over y, x), layer: 2 (over core).
Axes of the slice: x: 2, y: 2, z: 4, core: 2. Of those that a mesh axis runs over, the one named last changes fastest.
Arguments:
- basis: float32 [4096, 4096], P('row', 'col'), may hold values from -1 to 1, as said below
- basis_grad: float32 [4096, 4096], P('row', 'col'), may hold values from -768 to 768
- value_grad: float32 [4096], replicated, may hold values from -384 to 384
- ranks: int32 [4096], replicated, may hold values from 0 to 4095, each once
- offsets: int32 [4096], replicated, may hold values from 0 to 3
Outputs:
- grad_matrix: float32 [4096, 4096], P(('row', 'layer'), 'col')
Inputs may be any that keep to these rules, and one draw needn't show every extreme that they name: The columns of basis are orthonormal. ranks holds every number of 0 to 4095 once, so eigenvalues of different indices differ by 1 or more.
All inputs are finite; a program needn't handle non-finite values.
Results may differ from a plain program's by a relative error of at most 0.000098.
Values sent between devices are 32-bit elements; how exact they have to be, the bound alone decides.
A program may use at most 128 MiB of HBM per device.

v0:
```python
import jax
import jax.numpy as jnp
from jax import lax
from jax.sharding import PartitionSpec as P


def on_device(basis, basis_grad, value_grad, ranks, offsets):
    highest = lax.Precision.HIGHEST
    rows_blk, cols_blk = basis.shape
    layers = lax.axis_size("layer")
    row_id = lax.axis_index("row")
    col_id = lax.axis_index("col")
    layer_id = lax.axis_index("layer")
    half_rows = rows_blk // layers
    half_cols = cols_blk // layers
    u_top = lax.dynamic_slice_in_dim(basis, layer_id * half_rows, half_rows, 0)
    du_top = lax.dynamic_slice_in_dim(basis_grad, layer_id * half_rows, half_rows, 0)
    row_strip = lax.all_gather(u_top, "col", axis=1, tiled=True)
    mirrored = lax.all_to_all(row_strip, "row", split_axis=1, concat_axis=0, tiled=True)
    section = mirrored
    inner = lax.dot_general(
        section,
        lax.all_gather(du_top, "row", axis=0, tiled=True),
        (((0,), (0,)), ((), ())),
        precision=highest,
        preferred_element_type=jnp.float32,
    )
    inner_whole = lax.psum(inner, "layer")
    inner_half = lax.dynamic_slice_in_dim(inner_whole, layer_id * half_rows, half_rows, 0)
    eigen = 4.0 * ranks.astype(jnp.float32) + offsets.astype(jnp.float32)
    row_begin = row_id * rows_blk + layer_id * half_rows
    col_begin = col_id * cols_blk
    row_index = row_begin + jnp.arange(half_rows, dtype=jnp.int32)
    col_index = col_begin + jnp.arange(cols_blk, dtype=jnp.int32)
    eigen_rows = lax.dynamic_slice_in_dim(eigen, row_begin, half_rows, 0)
    eigen_cols = lax.dynamic_slice_in_dim(eigen, col_begin, cols_blk, 0)
    grad_cols = lax.dynamic_slice_in_dim(value_grad, col_begin, cols_blk, 0)
    on_diagonal = row_index[:, None] == col_index[None, :]
    spacing = eigen_cols[None, :] - eigen_rows[:, None]
    scaled = jnp.where(
        on_diagonal,
        grad_cols[None, :],
        inner_half / jnp.where(on_diagonal, jnp.float32(1.0), spacing),
    )
    u_right = lax.dynamic_slice_in_dim(basis, layer_id * half_cols, half_cols, 1)
    u_strip = lax.all_gather(u_right, "col", axis=1, tiled=True)
    section = u_strip
    left_prod = jnp.dot(
        section,
        lax.all_gather(scaled, "row", axis=0, tiled=True),
        precision=highest,
        preferred_element_type=jnp.float32,
    )
    left_whole = lax.psum(left_prod, "layer")
    left_half = lax.dynamic_slice_in_dim(left_whole, layer_id * half_cols, half_cols, 1)
    column_slab = lax.all_gather(u_right, "row", axis=0, tiled=True)
    far_rows = lax.all_to_all(column_slab, "col", split_axis=0, concat_axis=1, tiled=True)
    section = far_rows
    product = lax.dot_general(
        lax.all_gather(left_half, "col", axis=1, tiled=True),
        section,
        (((1,), (1,)), ((), ())),
        precision=highest,
        preferred_element_type=jnp.float32,
    )
    product_whole = lax.psum(product, "layer")
    return lax.dynamic_slice_in_dim(product_whole, layer_id * half_rows, half_rows, 0)


def solution(mesh):
    placed = (P("row", "col"), P("row", "col"), P(), P(), P())
    return jax.shard_map(
        on_device, mesh=mesh, in_specs=placed, out_specs=P(("row", "layer"), "col"), check_vma=False
    )
```

profile of v0, /device:TPU:0, one launch (start us, length us, event | category | flops | bytes accessed | tf_op | source)
XLA Modules:
  0.0 1150.9 jit_solution(15944361618842330479)
XLA Ops:
  7.4 0.0 all-gather.9.cloned.1.call-start
  7.4 1.7 constant_dynamic-slice_fusion.3
  9.1 1.8 copy.9
  10.9 0.0 all-gather.9.cloned.1.call-update
  10.9 90.4 %all-gather.9.cloned.1.call-done = f32[512,4096]{0,1:T(8,128)} async-done(((f32[512,1024]{0,1:T(8,128)}), f32[512,4096]{0,1:T(8,128)}) %all-gather.9.cloned.1.call-update) | async-done | bytes 8388624 | tf_op jit(solution)/shard_map/all_gather | solution.py:18
  101.3 5.7 all-to-all-start
  107.0 0.0 all-gather.11.cloned.1.call-start
  107.1 3.2 constant_dynamic-slice_fusion.2
  110.2 0.0 all-gather.11.cloned.1.call-update
  110.2 0.0 all-reduce.4.cloned.1.call-start
  110.3 314.7 %all-to-all-done = f32[512,4,1024]{0,2,1:T(8,128)} async-done(((f32[512,4,1024]{0,2,1:T(8,128)}), f32[512,4,1024]{0,2,1:T(8,128)}, u32[]{:S(2)}, u32[]{:S(2)}) %all-to-all-start) | async-done | bytes 8388640 | tf_op jit(solution)/shard_map/all_to_all | solution.py:19
  425.0 8.8 copy.7
  433.8 0.0 all-gather.11.cloned.1.call-done
  433.8 31.6 %fusion.1 = f32[1024,1024]{1,0:T(8,128)} fusion(f32[2048,1024]{1,0:T(8,128)} %bitcast.15, f32[2048,1024]{1,0:T(8,128)} %all-gather.11.cloned.1.call-done), kind=kOutput, calls=%fused_computation.11 | convolution fusion | flops 25769803776 | bytes 20971520 | tf_op jit(solution)/shard_map/dot_general | solution.py:21
  465.4 0.0 all-reduce.4.cloned.1.call-update
  465.4 0.0 copy-start
  465.5 0.0 copy-start.1
  465.5 0.0 all-gather.7.cloned.1.call-start
  465.5 3.1 constant_dynamic-slice_fusion.4
  468.6 0.0 all-gather.7.cloned.1.call-update
  468.6 0.0 all-gather.13.cloned.1.call-start
  468.7 0.0 copy-done
  468.7 0.0 copy-done.1
  468.7 0.1 dynamic_slice.33
  468.8 0.7 dynamic_slice.28
  469.5 22.3 %all-reduce.4.cloned.1.call-done = f32[1024,1024]{1,0:T(8,128)} async-done(((f32[1024,1024]{1,0:T(8,128)}), f32[1024,1024]{1,0:T(8,128)}) %all-reduce.4.cloned.1.call-update) | async-done | bytes 4194320 | tf_op jit(solution)/shard_map/psum | solution.py:28
  491.8 3.4 compare_select_fusion
  495.2 0.0 all-gather.13.cloned.1.call-update
  495.2 0.2 all-reduce.6.cloned.1.call-start
  495.5 86.9 %all-gather.7.cloned.1.call-done = f32[1024,2048]{1,0:T(8,128)} async-done(((f32[1024,512]{1,0:T(8,128)}), f32[1024,2048]{1,0:T(8,128)}) %all-gather.7.cloned.1.call-update) | async-done | bytes 8388624 | tf_op jit(solution)/shard_map/all_gather | solution.py:46
  582.4 151.1 %all-gather.13.cloned.1.call-done = f32[2048,1024]{1,0:T(8,128)} async-done(((f32[512,1024]{1,0:T(8,128)}), f32[2048,1024]{1,0:T(8,128)}) %all-gather.13.cloned.1.call-update) | async-done | bytes 8388624 | tf_op jit(solution)/shard_map/all_gather | solution.py:50
  733.4 31.8 %fusion.2 = f32[1024,1024]{1,0:T(8,128)} fusion(f32[1024,2048]{1,0:T(8,128)} %all-gather.7.cloned.1.call-done, f32[2048,1024]{1,0:T(8,128)} %all-gather.13.cloned.1.call-done), kind=kOutput, calls=%fused_computation.12 | convolution fusion | flops 25769803776 | bytes 20971520 | tf_op jit(solution)/shard_map/dot_general | solution.py:48
  765.3 0.0 all-reduce.6.cloned.1.call-update
  765.3 0.0 all-gather.17.cloned.1.call-start
  765.4 0.5 all-gather.17.cloned.1.call-update
  765.9 0.0 all-gather.15.cloned.1.call-start
  765.9 25.8 %all-reduce.6.cloned.1.call-done = f32[1024,1024]{1,0:T(8,128)} async-done(((f32[1024,1024]{1,0:T(8,128)}), f32[1024,1024]{1,0:T(8,128)}) %all-reduce.6.cloned.1.call-update) | async-done | bytes 4194320 | tf_op jit(solution)/shard_map/psum | solution.py:54
  791.7 3.2 constant_dynamic-slice_fusion.1
  794.9 0.0 all-gather.15.cloned.1.call-update
  794.9 0.0 all-reduce.8.cloned.1.call-start
  795.0 120.1 %all-gather.17.cloned.1.call-done = f32[4096,512]{1,0:T(8,128)} async-done(((f32[1024,512]{1,0:T(8,128)}), f32[4096,512]{1,0:T(8,128)}) %all-gather.17.cloned.1.call-update) | async-done | bytes 8388624 | tf_op jit(solution)/shard_map/all_gather | solution.py:56
  915.1 158.6 %all_to_all.38 = f32[4,1024,512]{2,1,0:T(8,128)} all-to-all(f32[4,1024,512]{2,1,0:T(8,128)} %bitcast.13), channel_id=1, replica_groups=mesh['row'=4,'col'=4,'layer'=2] {'col'}, dimensions={0} | all-to-all | bytes 16777216 | tf_op jit(solution)/shard_map/all_to_all | solution.py:57
  1073.7 8.7 copy.8
  1082.4 0.4 all-gather.15.cloned.1.call-done
  1082.8 31.8 %fusion.3 = f32[1024,1024]{1,0:T(8,128)} fusion(f32[1024,2048]{1,0:T(8,128)} %all-gather.15.cloned.1.call-done, f32[1024,2048]{0,1:T(8,128)} %bitcast.16), kind=kOutput, calls=%fused_computation.13 | convolution fusion | flops 25769803776 | bytes 20971520 | tf_op jit(solution)/shard_map/dot_general | solution.py:59
  1114.6 0.0 all-reduce.8.cloned.1.call-update
  1114.6 25.5 %all-reduce.8.cloned.1.call-done = f32[1024,1024]{1,0:T(8,128)} async-done(((f32[1024,1024]{1,0:T(8,128)}), f32[1024,1024]{1,0:T(8,128)}) %all-reduce.8.cloned.1.call-update) | async-done | bytes 4194320 | tf_op jit(solution)/shard_map/psum | solution.py:66
  1140.1 3.2 constant_dynamic-slice_fusion
  (4 shorter events, 0.0 us)
Async XLA Ops:
  7.4 93.9 %all-gather.9.cloned.1.call-start = ((), (), s32[]{:S(2)}) async-start(), calls=%async_computation.3 | async-start | bytes 10485760 | tf_op jit(solution)/shard_map/all_gather | solution.py:18
  101.3 323.7 %all-to-all-start = ((f32[512,4,1024]{0,2,1:T(8,128)}), f32[512,4,1024]{0,2,1:T(8,128)}, u32[]{:S(2)}, u32[]{:S(2)}) async-start(f32[512,4,1024]{0,2,1:T(8,128)} %bitcast.14), calls=%async_computation | async-start | bytes 16777216 | tf_op jit(solution)/shard_map/all_to_all | solution.py:19
  107.0 326.8 %all-gather.11.cloned.1.call-start = ((), (), s32[]{:S(2)}) async-start(), calls=%async_computation.4 | async-start | bytes 10485760 | tf_op jit(solution)/shard_map/all_gather | solution.py:23
  110.2 381.6 %all-reduce.4.cloned.1.call-start = ((), (), s32[]{:S(2)}) async-start(), calls=%async_computation.5 | async-start | bytes 8388608 | tf_op jit(solution)/shard_map/psum | solution.py:28
  465.4 3.2 copy-start
  465.5 3.2 copy-start.1
  465.5 116.9 %all-gather.7.cloned.1.call-start = ((), (), s32[]{:S(2)}) async-start(), calls=%async_computation.2 | async-start | bytes 10485760 | tf_op jit(solution)/shard_map/all_gather | solution.py:46
  468.6 264.8 %all-gather.13.cloned.1.call-start = ((), (), s32[]{:S(2)}) async-start(), calls=%async_computation.6 | async-start | bytes 10485760 | tf_op jit(solution)/shard_map/all_gather | solution.py:50
  495.2 296.5 %all-reduce.6.cloned.1.call-start = ((), (), s32[]{:S(2)}) async-start(), calls=%async_computation.7 | async-start | bytes 8388608 | tf_op jit(solution)/shard_map/psum | solution.py:54
  765.3 149.7 %all-gather.17.cloned.1.call-start = ((), (), s32[]{:S(2)}) async-start(), calls=%async_computation.9 | async-start | bytes 10485760 | tf_op jit(solution)/shard_map/all_gather | solution.py:56
  765.9 316.9 %all-gather.15.cloned.1.call-start = ((), (), s32[]{:S(2)}) async-start(), calls=%async_computation.8 | async-start | bytes 10485760 | tf_op jit(solution)/shard_map/all_gather | solution.py:60
  794.9 345.2 %all-reduce.8.cloned.1.call-start = ((), (), s32[]{:S(2)}) async-start(), calls=%async_computation.10 | async-start | bytes 8388608 | tf_op jit(solution)/shard_map/psum | solution.py:66
Sparse Core Ops, SparseCore 0:
  11.1 90.1 all-gather.8
  465.6 26.2 all-reduce.3
  493.7 88.6 all-gather.6
  583.8 149.5 all-gather.12
  765.4 26.2 all-reduce.5
  1114.8 25.3 all-reduce.7
Sparse Core Ops, SparseCore 1:
  110.3 293.4 all-gather.10
  767.4 147.6 all-gather.16
  916.8 165.9 all-gather.14
where the time goes:
time: 1150 us
  waiting for transfers between devices  838 us (73%)
  blocking collectives  159 us (14%)
  matrix products  95.3 us (8%)
  local copies, waits for them, and re-layouts  34.4 us (3%)
  between operations  15.2 us (1%)
    all_to_all x1, waiting for transfers between devices, on_device(): lax.all_to_all(row_strip, 'row', split_axis=1, concat_axis=0, tiled=True)  315 us
    all_to_all x1, blocking collectives, on_device(): lax.all_to_all(column_slab, 'col', split_axis=0, concat_axis=1, tiled=True)  159 us
    all_gather x1, waiting for transfers between devices, on_device(): lax.all_gather(scaled, 'row', axis=0, tiled=True)  151 us
    all_gather x1, waiting for transfers between devices, on_device(): column_slab = lax.all_gather(u_right, 'row', axis=0, tiled=True)  120 us
    all_gather x1, waiting for transfers between devices, on_device(): row_strip = lax.all_gather(u_top, 'col', axis=1, tiled=True)  90.4 us
    all_gather x1, waiting for transfers between devices, on_device(): u_strip = lax.all_gather(u_right, 'col', axis=1, tiled=True)  86.9 us
    dot_general x1, matrix products, on_device(): jnp.dot(section, lax.all_gather(scaled, 'row', axis=0, tiled=True), preci...  31.8 us
    dot_general x1, matrix products, on_device(): lax.dot_general(lax.all_gather(left_half, 'col', axis=1, tiled=True), sec...  31.8 us
  transfers between devices with their start and end apart: 10, of which 9 were waited for; matrix products, arithmetic and copies ran while one was open for 3% of the time, Pallas kernels for 0%

commit v1 on v0

--- a/solution.py
+++ b/solution.py
@@ -43,7 +43,12 @@
         inner_half / jnp.where(on_diagonal, jnp.float32(1.0), spacing),
     )
     u_right = lax.dynamic_slice_in_dim(basis, layer_id * half_cols, half_cols, 1)
-    u_strip = lax.all_gather(u_right, "col", axis=1, tiled=True)
+    ring = [u_right]
+    for hop in range(3):
+        ring.append(lax.ppermute(ring[-1], "col", [(dev, (dev + 1) % 4) for dev in range(4)]))
+    u_strip = jnp.roll(
+        jnp.concatenate(ring[::-1], axis=1), (lax.axis_index("col") + 1) * ring[0].shape[1], axis=1
+    )
     section = u_strip
     left_prod = jnp.dot(
         section,

time: 1150 us -> 1080 us (0.939)
  waiting for transfers between devices: 838 us -> 746 us
  local copies, waits for them, and re-layouts: 34.4 us -> 53.6 us
    all_gather x1, waiting for transfers between devices: 151 us -> 0.01 us  [on_device(): lax.all_gather(scaled, 'row', axis=0, tiled=True)]
    ppermute x0 -> x3, waiting for transfers between devices: none -> 142 us  [on_device(): lax.ppermute(ring[-1], 'col', [(dev, (dev + 1) % 4) for dev in range(4)])]
    all_gather x1 -> x0, waiting for transfers between devices: 86.9 us -> none  [on_device(): u_strip = lax.all_gather(u_right, 'col', axis=1, tiled=True)]
    unnamed x5 -> x20, local copies, waits for them, and re-layouts: 1.83 us -> 20.9 us
  transfers between devices with their start and end apart: 10 -> 12, of which waited for: 9 -> 10; matrix products, arithmetic and copies ran while one was open for 3% -> 4% of each run, Pallas kernels for 0% -> 0%
where the time goes in v1:
time: 1080 us
  waiting for transfers between devices  746 us (69%)
  blocking collectives  159 us (15%)
  matrix products  95.3 us (9%)
  local copies, waits for them, and re-layouts  53.6 us (5%)
  between operations  14.9 us (1%)
    all_to_all x1, waiting for transfers between devices, on_device(): lax.all_to_all(row_strip, 'row', split_axis=1, concat_axis=0, tiled=True)  315 us
    all_to_all x1, blocking collectives, on_device(): lax.all_to_all(column_slab, 'col', split_axis=0, concat_axis=1, tiled=True)  159 us
    ppermute x3, waiting for transfers between devices, on_device(): lax.ppermute(ring[-1], 'col', [(dev, (dev + 1) % 4) for dev in range(4)])  142 us
    all_gather x1, waiting for transfers between devices, on_device(): column_slab = lax.all_gather(u_right, 'row', axis=0, tiled=True)  120 us
    all_gather x1, waiting for transfers between devices, on_device(): row_strip = lax.all_gather(u_top, 'col', axis=1, tiled=True)  90.4 us
    dot_general x1, matrix products, on_device(): jnp.dot(section, lax.all_gather(scaled, 'row', axis=0, tiled=True), preci...  31.9 us
    dot_general x1, matrix products, on_device(): lax.dot_general(lax.all_gather(left_half, 'col', axis=1, tiled=True), sec...  31.8 us
    dot_general x1, matrix products, on_device(): lax.dot_general(section, lax.all_gather(du_top, 'row', axis=0, tiled=True...  31.6 us
  transfers between devices with their start and end apart: 12, of which 10 were waited for; matrix products, arithmetic and copies ran while one was open for 4% of the time, Pallas kernels for 0%

profile of v1, /device:TPU:0, one launch (start us, length us, event | category | flops | bytes accessed | tf_op | source)
XLA Modules:
  0.0 1080.7 jit_solution(4285743129014713352)
XLA Ops:
  7.4 1.7 constant_dynamic-slice_fusion.3
  9.1 1.8 copy.9
  10.9 90.4 %all-gather.6.cloned.1.call-done = f32[512,4096]{0,1:T(8,128)} async-done(((f32[512,1024]{0,1:T(8,128)}), f32[512,4096]{0,1:T(8,128)}) %all-gather.6.cloned.1.call-update) | async-done | bytes 8388624 | tf_op jit(solution)/shard_map/all_gather | solution.py:18
  101.3 5.7 all-to-all-start
  107.0 0.0 all-gather.8.cloned.1.call-start
  107.1 3.2 constant_dynamic-slice_fusion.2
  110.2 0.0 all-gather.8.cloned.1.call-update
  110.3 0.0 all-reduce.4.cloned.1.call-start
  110.3 314.7 %all-to-all-done = f32[512,4,1024]{0,2,1:T(8,128)} async-done(((f32[512,4,1024]{0,2,1:T(8,128)}), f32[512,4,1024]{0,2,1:T(8,128)}, u32[]{:S(2)}, u32[]{:S(2)}) %all-to-all-start) | async-done | bytes 8388640 | tf_op jit(solution)/shard_map/all_to_all | solution.py:19
  425.0 8.8 copy.7
  433.8 31.6 %fusion.4 = f32[1024,1024]{1,0:T(8,128)} fusion(f32[2048,1024]{1,0:T(8,128)} %bitcast.14, f32[2048,1024]{1,0:T(8,128)} %all-gather.8.cloned.1.call-done), kind=kOutput, calls=%fused_computation.22 | convolution fusion | flops 25769803776 | bytes 20971520 | tf_op jit(solution)/shard_map/dot_general | solution.py:21
  465.4 0.0 all-gather.10.cloned.1.call-start
  465.5 0.6 copy-done.4
  466.2 0.1 dynamic_slice.38
  466.2 0.7 dynamic_slice.33
  466.9 24.9 %all-reduce.4.cloned.1.call-done = f32[1024,1024]{1,0:T(8,128)} async-done(((f32[1024,1024]{1,0:T(8,128)}), f32[1024,1024]{1,0:T(8,128)}) %all-reduce.4.cloned.1.call-update) | async-done | bytes 4194320 | tf_op jit(solution)/shard_map/psum | solution.py:28
  491.8 3.4 compare_select_fusion
  495.2 0.0 all-gather.10.cloned.1.call-update
  495.3 0.0 all-reduce.6.cloned.1.call-start
  495.3 1.8 constant_dynamic-slice_fusion.4
  497.1 1.8 collective-permute-start
  498.9 47.0 %collective-permute-done = f32[1024,512]{1,0:T(8,128)S(1)} collective-permute-done((f32[1024,512]{1,0:T(8,128)S(1)}, f32[1024,512]{1,0:T(8,128)S(1)}, u32[]{:S(2)}, u32[]{:S(2)}) %collective-permute-start) | collective-permute-done | bytes 2097184 | tf_op jit(solution)/shard_map/ppermute | solution.py:48
  545.9 1.3 copy-done.2
  547.2 0.8 collective-permute-start.1
  548.0 47.3 %collective-permute-done.1 = f32[1024,512]{1,0:T(8,128)} collective-permute-done((f32[1024,512]{1,0:T(8,128)S(1)}, f32[1024,512]{1,0:T(8,128)}, u32[]{:S(2)}, u32[]{:S(2)}) %collective-permute-start.1) | collective-permute-done | bytes 2097184 | tf_op jit(solution)/shard_map/ppermute | solution.py:48
  595.3 47.4 %collective-permute-done.2 = f32[1024,512]{1,0:T(8,128)} collective-permute-done((f32[1024,512]{1,0:T(8,128)}, f32[1024,512]{1,0:T(8,128)}, u32[]{:S(2)}, u32[]{:S(2)}) %collective-permute-start.2) | collective-permute-done | bytes 2097184 | tf_op jit(solution)/shard_map/ppermute | solution.py:48
  642.7 3.1 constant_dynamic-update-slice_fusion.7
  645.8 3.2 constant_dynamic-update-slice_fusion.6
  649.0 1.5 constant_dynamic-update-slice_fusion.5
  650.5 1.5 constant_dynamic-update-slice_fusion.4
  652.1 3.1 constant_dynamic-update-slice_fusion.3
  655.2 3.2 constant_dynamic-update-slice_fusion.2
  658.3 1.5 constant_dynamic-update-slice_fusion.1
  659.9 1.5 constant_dynamic-update-slice_fusion
  661.4 31.9 %fusion = f32[1024,1024]{1,0:T(8,128)} fusion(f32[2048,1024]{1,0:T(8,128)} %all-gather.10.cloned.1.call-done, f32[1024,4096]{1,0:T(8,128)} %constant_dynamic-update-slice_fusion, s32[]{:T(128)S(6)} %select_n.38), kind=kOutput, calls=%fused_computation | convolution fusion | flops 25769803776 | bytes 20971524 | tf_op jit(solution)/shard_map/dot_general | solution.py:53
  693.3 0.0 all-gather.14.cloned.1.call-start
  693.3 0.5 all-gather.14.cloned.1.call-update
  693.9 0.0 all-gather.12.cloned.1.call-start
  693.9 28.0 %all-reduce.6.cloned.1.call-done = f32[1024,1024]{1,0:T(8,128)} async-done(((f32[1024,1024]{1,0:T(8,128)}), f32[1024,1024]{1,0:T(8,128)}) %all-reduce.6.cloned.1.call-update) | async-done | bytes 4194320 | tf_op jit(solution)/shard_map/psum | solution.py:59
  721.9 3.1 constant_dynamic-slice_fusion.1
  725.1 0.0 all-reduce.8.cloned.1.call-start
  725.1 120.0 %all-gather.14.cloned.1.call-done = f32[4096,512]{1,0:T(8,128)} async-done(((f32[1024,512]{1,0:T(8,128)}), f32[4096,512]{1,0:T(8,128)}) %all-gather.14.cloned.1.call-update) | async-done | bytes 8388624 | tf_op jit(solution)/shard_map/all_gather | solution.py:61
  845.1 158.6 %all_to_all.38 = f32[4,1024,512]{2,1,0:T(8,128)} all-to-all(f32[4,1024,512]{2,1,0:T(8,128)} %bitcast.12), channel_id=1, replica_groups=mesh['row'=4,'col'=4,'layer'=2] {'col'}, dimensions={0} | all-to-all | bytes 16777216 | tf_op jit(solution)/shard_map/all_to_all | solution.py:62
  1003.7 8.7 copy.8
  1012.4 0.4 all-gather.12.cloned.1.call-done
  1012.8 31.8 %fusion.5 = f32[1024,1024]{1,0:T(8,128)} fusion(f32[1024,2048]{1,0:T(8,128)} %all-gather.12.cloned.1.call-done, f32[1024,2048]{0,1:T(8,128)} %bitcast.15), kind=kOutput, calls=%fused_computation.23 | convolution fusion | flops 25769803776 | bytes 20971520 | tf_op jit(solution)/shard_map/dot_general | solution.py:64
  1044.7 25.5 %all-reduce.8.cloned.1.call-done = f32[1024,1024]{1,0:T(8,128)} async-done(((f32[1024,1024]{1,0:T(8,128)}), f32[1024,1024]{1,0:T(8,128)}) %all-reduce.8.cloned.1.call-update) | async-done | bytes 4194320 | tf_op jit(solution)/shard_map/psum | solution.py:71
  1070.2 3.2 constant_dynamic-slice_fusion
  (23 shorter events, 0.1 us)
Async XLA Ops:
  7.4 93.9 %all-gather.6.cloned.1.call-start = ((), (), s32[]{:S(2)}) async-start(), calls=%async_computation.2 | async-start | bytes 10485760 | tf_op jit(solution)/shard_map/all_gather | solution.py:18
  101.3 323.7 %all-to-all-start = ((f32[512,4,1024]{0,2,1:T(8,128)}), f32[512,4,1024]{0,2,1:T(8,128)}, u32[]{:S(2)}, u32[]{:S(2)}) async-start(f32[512,4,1024]{0,2,1:T(8,128)} %bitcast.13), calls=%async_computation | async-start | bytes 16777216 | tf_op jit(solution)/shard_map/all_to_all | solution.py:19
  107.0 326.8 %all-gather.8.cloned.1.call-start = ((), (), s32[]{:S(2)}) async-start(), calls=%async_computation.3 | async-start | bytes 10485760 | tf_op jit(solution)/shard_map/all_gather | solution.py:23
  110.3 381.6 %all-reduce.4.cloned.1.call-start = ((), (), s32[]{:S(2)}) async-start(), calls=%async_computation.4 | async-start | bytes 8388608 | tf_op jit(solution)/shard_map/psum | solution.py:28
  465.4 0.7 copy-start.4
  465.4 0.7 copy-start.5
  465.4 195.9 %all-gather.10.cloned.1.call-start = ((), (), s32[]{:S(2)}) async-start(), calls=%async_computation.5 | async-start | bytes 10485760 | tf_op jit(solution)/shard_map/all_gather | solution.py:55
  495.3 226.7 %all-reduce.6.cloned.1.call-start = ((), (), s32[]{:S(2)}) async-start(), calls=%async_computation.6 | async-start | bytes 8388608 | tf_op jit(solution)/shard_map/psum | solution.py:59
  497.1 152.0 %copy-start.1 = (f32[1024,512]{1,0:T(8,128)}, f32[1024,512]{1,0:T(8,128)S(1)}, u32[]{:S(2)}) copy-start(f32[1024,512]{1,0:T(8,128)S(1)} %constant_dynamic-slice_fusion.4) | copy-start | bytes 6291460
  497.1 48.8 %collective-permute-start = (f32[1024,512]{1,0:T(8,128)S(1)}, f32[1024,512]{1,0:T(8,128)S(1)}, u32[]{:S(2)}, u32[]{:S(2)}) collective-permute-start(f32[1024,512]{1,0:T(8,128)S(1)} %constant_dynamic-slice_fusion.4), channel_id=1, source_target_pairs={{0,2},{2,4},{4,6},{6,0},{1,3},{3,5},{5,7},{7,1},{8,10},{10,12},{12... | collective-permute-start | bytes 6291464 | tf_op jit(solution)/shard_map/ppermute | solution.py:48
  545.9 1.3 copy-start.2
  547.2 48.1 %collective-permute-start.1 = (f32[1024,512]{1,0:T(8,128)S(1)}, f32[1024,512]{1,0:T(8,128)}, u32[]{:S(2)}, u32[]{:S(2)}) collective-permute-start(f32[1024,512]{1,0:T(8,128)S(1)} %collective-permute-done), channel_id=1, source_target_pairs={{0,2},{2,4},{4,6},{6,0},{1,3},{3,5},{5,7},{7,1},{8,10},{10,12},{12... | collective-permute-start | bytes 6291464 | tf_op jit(solution)/shard_map/ppermute | solution.py:48
  595.3 47.4 %collective-permute-start.2 = (f32[1024,512]{1,0:T(8,128)}, f32[1024,512]{1,0:T(8,128)}, u32[]{:S(2)}, u32[]{:S(2)}) collective-permute-start(f32[1024,512]{1,0:T(8,128)} %collective-permute-done.1), channel_id=1, source_target_pairs={{0,2},{2,4},{4,6},{6,0},{1,3},{3,5},{5,7},{7,1},{8,10},{10,12},{12... | collective-permute-start | bytes 6291464 | tf_op jit(solution)/shard_map/ppermute | solution.py:48
  595.3 53.7 %copy-start.3 = (f32[1024,512]{1,0:T(8,128)S(1)}, f32[1024,512]{1,0:T(8,128)}, u32[]{:S(2)}) copy-start(f32[1024,512]{1,0:T(8,128)} %copy-done.2) | copy-start | bytes 6291460
  645.8 4.7 copy-start
  693.3 151.8 %all-gather.14.cloned.1.call-start = ((), (), s32[]{:S(2)}) async-start(), calls=%async_computation.8 | async-start | bytes 10485760 | tf_op jit(solution)/shard_map/all_gather | solution.py:61
  693.9 318.9 %all-gather.12.cloned.1.call-start = ((), (), s32[]{:S(2)}) async-start(), calls=%async_computation.7 | async-start | bytes 10485760 | tf_op jit(solution)/shard_map/all_gather | solution.py:65
  725.1 345.1 %all-reduce.8.cloned.1.call-start = ((), (), s32[]{:S(2)}) async-start(), calls=%async_computation.9 | async-start | bytes 8388608 | tf_op jit(solution)/shard_map/psum | solution.py:71
Sparse Core Ops, SparseCore 0:
  11.1 90.1 all-gather.5
  465.6 26.2 all-reduce.3
  693.4 28.4 all-reduce.5
  1044.8 25.3 all-reduce.7
Sparse Core Ops, SparseCore 1:
  110.3 293.4 all-gather.7
  495.3 150.6 all-gather.9
  695.3 149.7 all-gather.13
  847.0 165.8 all-gather.11
